TPU v7x, 32 devices: a whole 2x2x4 slice. The times are simulated.
32 devices in a mesh: expert: 4 (over x, core), shard: 8 (over z, y).
Axes of the slice: x: 2, y: 2, z: 4, core: 2. Of those that a mesh axis runs over, the one named last changes fastest.
Arguments:
- w_gate: float32 [64, 2048, 1408], P('expert', 'shard'), may hold values from -0.1875 to 0.1875
- w_up: float32 [64, 2048, 1408], P('expert', 'shard'), may hold values from -0.1875 to 0.1875
- router_weight: float32 [2048, 64], P('shard', 'expert'), may hold values from -0.125 to 0.125
- router_gain: float32 [2048], P('shard'), may hold values from 0.25 to 1.75
Outputs:
- serve_gate: bfloat16 [64, 2048, 1408], P('expert', None, 'shard')
- serve_up: bfloat16 [64, 2048, 1408], P('expert', None, 'shard')
- scale_gate: float32 [64, 1408], P('expert', 'shard')
- scale_up: float32 [64, 1408], P('expert', 'shard')
- serve_router: bfloat16 [2048, 64], replicated
All inputs are finite; a program needn't handle non-finite values. Where the computation divides by a largest or mean magnitude, that divisor is 1e-20 or more.
Results may differ from a plain program's by a relative error of at most 0.001.
Values may be sent and summed in bfloat16 or wider, within the bound.
A program may use at most 192 MiB of HBM per device.

v0:
```python
import jax
import jax.numpy as jnp
from jax import lax
from jax.sharding import PartitionSpec as P

D_MODEL = 2048


def on_device(w_gate, w_up, router_weight, router_gain):
    total_gate, total_up = lax.psum(
        (jnp.sum(jnp.abs(w_gate), axis=1), jnp.sum(jnp.abs(w_up), axis=1)), "shard"
    )
    scale_gate = total_gate / D_MODEL
    scale_up = total_up / D_MODEL
    narrow_gate, narrow_up = (
        (w_gate / jnp.expand_dims(scale_gate, 1)).astype(jnp.bfloat16),
        (w_up / jnp.expand_dims(scale_up, 1)).astype(jnp.bfloat16),
    )
    serve_gate, serve_up = (
        lax.all_to_all(narrow_gate, "shard", split_axis=2, concat_axis=1, tiled=True),
        lax.all_to_all(narrow_up, "shard", split_axis=2, concat_axis=1, tiled=True),
    )
    scale_gate = lax.dynamic_slice_in_dim(
        scale_gate, lax.axis_index("shard") * serve_gate.shape[2], serve_gate.shape[2], axis=1
    )
    scale_up = lax.dynamic_slice_in_dim(
        scale_up, lax.axis_index("shard") * serve_up.shape[2], serve_up.shape[2], axis=1
    )
    part_router = (router_weight * router_gain[:, None]).astype(jnp.bfloat16)
    row_router = lax.all_gather(part_router, "shard", axis=0, tiled=True)
    serve_router = lax.all_gather(row_router, "expert", axis=1, tiled=True)
    return (serve_gate, serve_up, scale_gate, scale_up, serve_router)


def solution(mesh):
    placed = (
        P("expert", "shard", None),
        P("expert", "shard", None),
        P("shard", "expert"),
        P("shard"),
    )
    return jax.shard_map(
        on_device,
        mesh=mesh,
        in_specs=placed,
        out_specs=(
            P("expert", None, "shard"),
            P("expert", None, "shard"),
            P("expert", "shard"),
            P("expert", "shard"),
            P(),
        ),
        check_vma=False,
    )
```

profile of v0, /device:TPU:0, one launch (start us, length us, event | category | flops | bytes accessed | tf_op | source)
XLA Modules:
  0.0 714.1 jit_solution(9484981068573006527)
XLA Ops:
  7.2 0.0 all-reduce.3.cloned.1.call-start
  7.2 16.0 %abs_reduce_fusion = (f32[16,1408]{1,0:T(8,128)}, f32[16,1408]{1,0:T(8,128)}) fusion(f32[16,256,1408]{2,1,0:T(8,128)} %param.5, f32[16,256,1408]{2,1,0:T(8,128)} %param.4), kind=kLoop, calls=%fused_computation.1 | loop fusion | flops 23023616 | bytes 46317568 | tf_op jit(solution)/shard_map/reduce_sum | solution.py:11
  23.3 0.0 all-reduce.3.cloned.1.call-update
  23.3 23.7 %copy.22 = f32[16,256,1408]{1,0,2:T(8,128)} copy(f32[16,256,1408]{2,1,0:T(8,128)} %param.5) | data formatting | bytes 46137344 | tf_op args[1]
  47.0 50.0 %all-reduce.3.cloned.1.call-done = (f32[16,1408]{1,0:T(8,128)}, f32[16,1408]{1,0:T(8,128)}) async-done(((f32[16,1408]{1,0:T(8,128)}, f32[16,1408]{1,0:T(8,128)}), (f32[16,1408]{1,0:T(8,128)}, f32[16,1408]{1,0:T(8,128)})) %all-reduce.3.cloned.1.call-update) | async-done | bytes 180240 | tf_op jit(solution)/shard_map/psum | solution.py:10
  97.0 0.9 broadcast_multiply_fusion
  97.9 0.3 copy.21
  98.1 14.2 %divide_convert_fusion = bf16[16,256,1408]{1,0,2:T(8,128)(2,1)} fusion(f32[16,256,1408]{1,0,2:T(8,128)} %copy.22, f32[16,1408]{0,1:T(8,128)S(1)} %copy.21), kind=kLoop, calls=%fused_computation | loop fusion | flops 11534336 | bytes 34693120 | tf_op jit(solution)/shard_map/convert_element_type | solution.py:17
  112.4 5.2 all-to-all-start.1
  117.6 0.0 copy-start
  117.6 23.7 %copy.18 = f32[16,256,1408]{1,0,2:T(8,128)} copy(f32[16,256,1408]{2,1,0:T(8,128)} %param.4) | data formatting | bytes 46137344 | tf_op args[0]
  141.3 0.0 copy-done
  141.3 0.3 copy.17
  141.6 0.0 copy-start.1
  141.6 0.0 copy-start.2
  141.6 14.2 %divide_convert_fusion.1 = bf16[16,256,1408]{1,0,2:T(8,128)(2,1)} fusion(f32[16,256,1408]{1,0,2:T(8,128)} %copy.18, f32[16,1408]{0,1:T(8,128)S(1)} %copy.17), kind=kLoop, calls=%fused_computation.2 | loop fusion | flops 11534336 | bytes 34693120 | tf_op jit(solution)/shard_map/convert_element_type | solution.py:16
  155.8 210.5 %all-to-all-done.1 = bf16[16,256,1408]{1,0,2:T(8,128)(2,1)} async-done(((bf16[16,256,1408]{1,0,2:T(8,128)(2,1)}), bf16[16,256,1408]{1,0,2:T(8,128)(2,1)}, u32[]{:S(2)}, u32[]{:S(2)}) %all-to-all-start.1) | async-done | bytes 11534368 | tf_op jit(solution)/shard_map/all_to_all | solution.py:21
  366.4 5.3 all-to-all-start
  371.7 0.0 copy-done.1
  371.7 0.0 copy-done.2
  371.7 269.1 %all_gather.6 = bf16[2048,16]{0,1:T(8,128)(2,1)S(1)} all-gather(bf16[256,16]{0,1:T(8,128)(2,1)S(1)} %multiply_convert_fusion), channel_id=1, replica_groups=mesh['expert'=4,'shard'=8] {'shard'}, dimensions={0}, use_global_device_ids=true | all-gather | bytes 73728 | tf_op jit(solution)/shard_map/all_gather | solution.py:30
  640.8 5.8 all_gather.7
  646.6 0.7 constant_dynamic-slice_fusion
  647.3 0.7 constant_dynamic-slice_fusion.1
  647.9 11.4 %copy.24 = bf16[16,8,256,176]{2,1,3,0:T(8,128)(2,1)} copy(bf16[16,8,256,176]{2,0,3,1:T(8,128)(2,1)} %bitcast.5) | data formatting | bytes 23068672 | tf_op jit(solution)/shard_map/all_to_all | solution.py:21
  659.3 18.0 %all_to_all.33 = bf16[16,2048,176]{1,2,0:T(8,128)(2,1)} reshape(bf16[16,8,256,176]{2,1,3,0:T(8,128)(2,1)} %copy.24) | data formatting | bytes 23068672 | tf_op jit(solution)/shard_map/all_to_all | solution.py:21
  677.3 0.0 all-to-all-done
  677.3 11.4 %copy.20 = bf16[16,8,256,176]{2,1,3,0:T(8,128)(2,1)} copy(bf16[16,8,256,176]{2,0,3,1:T(8,128)(2,1)} %bitcast.2) | data formatting | bytes 23068672 | tf_op jit(solution)/shard_map/all_to_all | solution.py:20
  688.6 18.0 %all_to_all.29 = bf16[16,2048,176]{1,2,0:T(8,128)(2,1)} reshape(bf16[16,8,256,176]{2,1,3,0:T(8,128)(2,1)} %copy.20) | data formatting | bytes 23068672 | tf_op jit(solution)/shard_map/all_to_all | solution.py:20
  706.6 0.7 copy.30
  (2 shorter events, 0.0 us)
Async XLA Ops:
  7.2 89.8 %all-reduce.3.cloned.1.call-start = ((), (), s32[]{:S(2)}) async-start(), calls=%async_computation.2 | async-start | bytes 360448 | tf_op jit(solution)/shard_map/psum | solution.py:10
  112.4 254.0 %all-to-all-start.1 = ((bf16[16,256,1408]{1,0,2:T(8,128)(2,1)}), bf16[16,256,1408]{1,0,2:T(8,128)(2,1)}, u32[]{:S(2)}, u32[]{:S(2)}) async-start(bf16[16,256,1408]{1,0,2:T(8,128)(2,1)} %divide_convert_fusion), calls=%async_computation.1 | async-start | bytes 23068672 | tf_op jit(solution)/shard_map/all_to_all | solution.py:21
  117.6 23.7 %copy-start = (f32[16,1408]{1,0:T(8,128)S(1)}, f32[16,1408]{1,0:T(8,128)}, u32[]{:S(2)}) copy-start(f32[16,1408]{1,0:T(8,128)} %get-tuple-element.5) | copy-start | bytes 270340
  141.6 230.1 %copy-start.1 = (f32[256,16]{0,1:T(8,128)S(1)}, f32[256,16]{0,1:T(8,128)}, u32[]{:S(2)}) copy-start(f32[256,16]{0,1:T(8,128)} %param.6) | copy-start | bytes 49156
  141.6 230.1 %copy-start.2 = (f32[256]{0:T(256)S(1)}, f32[256]{0:T(256)}, u32[]{:S(2)}) copy-start(f32[256]{0:T(256)} %param.7) | copy-start | bytes 3076
  366.4 310.9 %all-to-all-start = ((bf16[16,256,1408]{1,0,2:T(8,128)(2,1)}), bf16[16,256,1408]{1,0,2:T(8,128)(2,1)}, u32[]{:S(2)}, u32[]{:S(2)}) async-start(bf16[16,256,1408]{1,0,2:T(8,128)(2,1)} %divide_convert_fusion.1), calls=%async_computation | async-start | bytes 23068672 | tf_op jit(solution)/shard_map/all_to_all | solution.py:20
Sparse Core Ops, SparseCore 0:
  23.4 73.5 all-reduce.2
where the time goes:
time: 716 us; the launch traced here: 714 us
  blocking collectives  275 us (38%)
  waiting for transfers between devices  261 us (36%)
  local copies, waits for them, and re-layouts  109 us (15%)
  other arithmetic  45.4 us (6%)
  between operations  14.1 us (2%)
  starting transfers between devices  10.5 us (1%)
    all_gather x1, blocking collectives, on_device(): row_router = lax.all_gather(part_router, 'shard', axis=0, tiled=True)  269 us
    all_to_all x1, waiting for transfers between devices, on_device(): lax.all_to_all(narrow_up, 'shard', split_axis=2, concat_axis=1, tiled=True)  211 us
    psum x1, waiting for transfers between devices, on_device(): lax.psum((jnp.sum(jnp.abs(w_gate), axis=1), jnp.sum(jnp.abs(w_up), axis=1...  50 us
    unnamed x9, local copies, waits for them, and re-layouts  48.1 us
    all_to_all x2, local copies, waits for them, and re-layouts, on_device(): lax.all_to_all(narrow_gate, 'shard', split_axis=2, concat_axis=1, tiled=T...  29.3 us
    all_to_all x2, local copies, waits for them, and re-layouts, on_device(): lax.all_to_all(narrow_up, 'shard', split_axis=2, concat_axis=1, tiled=True)  29.3 us
    reduce_sum x1, other arithmetic, on_device(): jnp.sum(jnp.abs(w_up), axis=1)  16 us
  transfers between devices with their start and end apart: 3, of which 2 were waited for; matrix products, arithmetic and copies ran while one was open for 10% of the time, Pallas kernels for 0%

commit v1 on v0

--- a/solution.py
+++ b/solution.py
@@ -18,7 +18,12 @@
     )
     serve_gate, serve_up = (
         lax.all_to_all(narrow_gate, "shard", split_axis=2, concat_axis=1, tiled=True),
-        lax.all_to_all(narrow_up, "shard", split_axis=2, concat_axis=1, tiled=True),
+        jnp.concatenate(
+            lax.all_to_all(
+                jnp.stack(jnp.split(narrow_up, lax.axis_size("shard"), axis=2)), "shard", 0, 0
+            ),
+            axis=1,
+        ),
     )
     scale_gate = lax.dynamic_slice_in_dim(
         scale_gate, lax.axis_index("shard") * serve_gate.shape[2], serve_gate.shape[2], axis=1

time: 716 us -> 697 us (0.973)
  local copies, waits for them, and re-layouts: 109 us -> 98.4 us
    all_to_all x1, waiting for transfers between devices: 211 us -> 0.01 us  [on_device(): lax.all_to_all(jnp.stack(jnp.split(narrow_up, lax.axis_size('shard'), axi...]
    all_to_all x1, waiting for transfers between devices: 0.01 us -> 206 us  [on_device(): lax.all_to_all(narrow_gate, 'shard', split_axis=2, concat_axis=1, tiled=T...]
    all_to_all x2 -> x0, local copies, waits for them, and re-layouts: 29.3 us -> none  [on_device(): lax.all_to_all(narrow_up, 'shard', split_axis=2, concat_axis=1, tiled=True)]
    reshape x0 -> x1, local copies, waits for them, and re-layouts: none -> 10 us  [on_device(): jnp.concatenate(lax.all_to_all(jnp.stack(jnp.split(narrow_up, lax.axis_si...]
    unnamed x9 -> x16, local copies, waits for them, and re-layouts: 48.1 us -> 56.2 us
  transfers between devices with their start and end apart: 3 -> 3, of which waited for: 2 -> 2; matrix products, arithmetic and copies ran while one was open for 10% -> 11% of each run, Pallas kernels for 0% -> 0%
where the time goes in v1:
time: 697 us; the launch traced here: 695 us
  blocking collectives  275 us (39%)
  waiting for transfers between devices  256 us (37%)
  local copies, waits for them, and re-layouts  98.4 us (14%)
  other arithmetic  41 us (6%)
  between operations  14.1 us (2%)
  starting transfers between devices  10.5 us (2%)
    all_gather x1, blocking collectives, on_device(): row_router = lax.all_gather(part_router, 'shard', axis=0, tiled=True)  269 us
    all_to_all x1, waiting for transfers between devices, on_device(): lax.all_to_all(narrow_gate, 'shard', split_axis=2, concat_axis=1, tiled=T...  206 us
    unnamed x16, local copies, waits for them, and re-layouts  56.2 us
    psum x1, waiting for transfers between devices, on_device(): lax.psum((jnp.sum(jnp.abs(w_gate), axis=1), jnp.sum(jnp.abs(w_up), axis=1...  50 us
    all_to_all x2, local copies, waits for them, and re-layouts, on_device(): lax.all_to_all(narrow_gate, 'shard', split_axis=2, concat_axis=1, tiled=T...  29.3 us
    reduce_sum x1, other arithmetic, on_device(): jnp.sum(jnp.abs(w_up), axis=1)  16 us
    convert_element_type x1, other arithmetic, on_device(): (w_gate / jnp.expand_dims(scale_gate, 1)).astype(jnp.bfloat16)  14.2 us
  transfers between devices with their start and end apart: 3, of which 2 were waited for; matrix products, arithmetic and copies ran while one was open for 11% of the time, Pallas kernels for 0%

profile of v1, /device:TPU:0, one launch (start us, length us, event | category | flops | bytes accessed | tf_op | source)
XLA Modules:
  0.0 694.8 jit_solution(5658346022208422891)
XLA Ops:
  7.2 0.0 all-reduce.3.cloned.1.call-start
  7.2 16.0 %abs_reduce_fusion = (f32[16,1408]{1,0:T(8,128)}, f32[16,1408]{1,0:T(8,128)}) fusion(f32[16,256,1408]{2,1,0:T(8,128)} %param.5, f32[16,256,1408]{2,1,0:T(8,128)} %param.4), kind=kLoop, calls=%fused_computation.1 | loop fusion | flops 23023616 | bytes 46317568 | tf_op jit(solution)/shard_map/reduce_sum | solution.py:11
  23.3 0.0 all-reduce.3.cloned.1.call-update
  23.3 23.7 %copy.22 = f32[16,256,1408]{1,0,2:T(8,128)} copy(f32[16,256,1408]{2,1,0:T(8,128)} %param.4) | data formatting | bytes 46137344 | tf_op args[0]
  47.0 50.0 %all-reduce.3.cloned.1.call-done = (f32[16,1408]{1,0:T(8,128)}, f32[16,1408]{1,0:T(8,128)}) async-done(((f32[16,1408]{1,0:T(8,128)}, f32[16,1408]{1,0:T(8,128)}), (f32[16,1408]{1,0:T(8,128)}, f32[16,1408]{1,0:T(8,128)})) %all-reduce.3.cloned.1.call-update) | async-done | bytes 180240 | tf_op jit(solution)/shard_map/psum | solution.py:10
  97.0 0.9 broadcast_multiply_fusion.1
  97.9 0.3 copy.21
  98.1 14.2 %divide_convert_fusion.1 = bf16[16,256,1408]{1,0,2:T(8,128)(2,1)} fusion(f32[16,256,1408]{1,0,2:T(8,128)} %copy.22, f32[16,1408]{0,1:T(8,128)S(1)} %copy.21), kind=kLoop, calls=%fused_computation.2 | loop fusion | flops 11534336 | bytes 34693120 | tf_op jit(solution)/shard_map/convert_element_type | solution.py:16
  112.4 5.2 all-to-all-start
  117.6 0.0 copy-start
  117.6 23.4 %copy.25 = f32[16,256,1408]{1,2,0:T(8,128)} copy(f32[16,256,1408]{2,1,0:T(8,128)} %param.5) | data formatting | bytes 46137344 | tf_op args[1]
  141.0 0.0 copy-done
  141.0 9.8 %divide_convert_fusion = bf16[16,256,1408]{1,2,0:T(8,128)(2,1)S(1)} fusion(f32[16,256,1408]{1,2,0:T(8,128)} %copy.25, f32[16,1408]{1,0:T(8,128)S(1)} %broadcast_multiply_fusion), kind=kLoop, calls=%fused_computation | loop fusion | flops 11534336 | bytes 34693120 | tf_op jit(solution)/shard_map/convert_element_type | solution.py:17
  150.8 1.2 fusion.7
  152.0 1.2 fusion.6
  153.3 1.2 fusion.5
  154.5 1.2 fusion.4
  155.7 1.2 fusion.3
  156.9 1.2 fusion.2
  158.1 1.2 fusion.1
  159.3 1.2 fusion
  160.5 0.0 copy-start.1
  160.5 0.0 copy-start.2
  160.5 205.9 %all-to-all-done = bf16[16,256,1408]{1,0,2:T(8,128)(2,1)} async-done(((bf16[16,256,1408]{1,0,2:T(8,128)(2,1)}), bf16[16,256,1408]{1,0,2:T(8,128)(2,1)}, u32[]{:S(2)}, u32[]{:S(2)}) %all-to-all-start) | async-done | bytes 11534368 | tf_op jit(solution)/shard_map/all_to_all | solution.py:20
  366.4 5.3 all-to-all-start.1
  371.7 0.0 copy-done.1
  371.7 0.0 copy-done.2
  371.7 269.1 %all_gather.6 = bf16[2048,16]{0,1:T(8,128)(2,1)S(1)} all-gather(bf16[256,16]{0,1:T(8,128)(2,1)S(1)} %multiply_convert_fusion), channel_id=1, replica_groups=mesh['expert'=4,'shard'=8] {'shard'}, dimensions={0}, use_global_device_ids=true | all-gather | bytes 73728 | tf_op jit(solution)/shard_map/all_gather | solution.py:35
  640.8 5.8 all_gather.7
  646.6 0.7 constant_dynamic-slice_fusion.1
  647.3 0.7 constant_dynamic-slice_fusion
  647.9 11.3 %copy.24 = bf16[16,8,256,176]{2,1,3,0:T(8,128)(2,1)} copy(bf16[16,8,256,176]{2,0,3,1:T(8,128)(2,1)} %bitcast.2) | data formatting | bytes 23068672 | tf_op jit(solution)/shard_map/all_to_all | solution.py:20
  659.3 18.0 %all_to_all.19 = bf16[16,2048,176]{1,2,0:T(8,128)(2,1)} reshape(bf16[16,8,256,176]{2,1,3,0:T(8,128)(2,1)} %copy.24) | data formatting | bytes 23068672 | tf_op jit(solution)/shard_map/all_to_all | solution.py:20
  677.2 0.0 all-to-all-done.1
  677.2 10.0 %copy.28 = bf16[8,16,22,8,256]{4,3,0,2,1:T(8,128)(2,1)} copy(bf16[8,16,22,8,256]{4,3,2,1,0:T(8,128)(2,1)} %bitcast.12) | data formatting | bytes 23068672 | tf_op jit(solution)/shard_map/reshape | solution.py:21
  687.2 0.7 copy.39
  (2 shorter events, 0.0 us)
Async XLA Ops:
  7.2 89.8 %all-reduce.3.cloned.1.call-start = ((), (), s32[]{:S(2)}) async-start(), calls=%async_computation.2 | async-start | bytes 360448 | tf_op jit(solution)/shard_map/psum | solution.py:10
  112.4 254.0 %all-to-all-start = ((bf16[16,256,1408]{1,0,2:T(8,128)(2,1)}), bf16[16,256,1408]{1,0,2:T(8,128)(2,1)}, u32[]{:S(2)}, u32[]{:S(2)}) async-start(bf16[16,256,1408]{1,0,2:T(8,128)(2,1)} %divide_convert_fusion.1), calls=%async_computation | async-start | bytes 23068672 | tf_op jit(solution)/shard_map/all_to_all | solution.py:20
  117.6 23.4 %copy-start = (f32[16,1408]{1,0:T(8,128)S(1)}, f32[16,1408]{1,0:T(8,128)}, u32[]{:S(2)}) copy-start(f32[16,1408]{1,0:T(8,128)} %get-tuple-element.6) | copy-start | bytes 270340
  160.5 211.2 %copy-start.1 = (f32[256,16]{0,1:T(8,128)S(1)}, f32[256,16]{0,1:T(8,128)}, u32[]{:S(2)}) copy-start(f32[256,16]{0,1:T(8,128)} %param.6) | copy-start | bytes 49156
  160.5 211.2 %copy-start.2 = (f32[256]{0:T(256)S(1)}, f32[256]{0:T(256)}, u32[]{:S(2)}) copy-start(f32[256]{0:T(256)} %param.7) | copy-start | bytes 3076
  366.4 310.9 %all-to-all-start.1 = ((bf16[8,16,256,176]{2,3,1,0:T(8,128)(2,1)}), bf16[8,16,256,176]{2,3,1,0:T(8,128)(2,1)}, u32[]{:S(2)}, u32[]{:S(2)}) async-start(bf16[8,16,256,176]{2,3,1,0:T(8,128)(2,1)} %fusion), calls=%async_computation.1 | async-start | bytes 23068672 | tf_op jit(solution)/shard_map/all_to_all | solution.py:22
Sparse Core Ops, SparseCore 0:
  23.4 73.5 all-reduce.2
